TPU v7x, 32 devices: a whole 2x2x4 slice. The times are simulated.
32 devices in a mesh: pts: 16 (over z, x, core), bond: 2 (over y).
Axes of the slice: x: 2, y: 2, z: 4, core: 2. Of those that a mesh axis runs over, the one named last changes fastest.
Arguments:
- displacement: float32 [3, 64, 64, 256], P(None, 'pts', 'bond'), may hold values from -1.5 to 1.5
- velocity: float32 [3, 64, 64, 256], P(None, 'pts', 'bond'), may hold values from -6 to 6
- stiffness: float32 [64, 64, 256], P('pts', 'bond'), may hold values from 0.5 to 8
- offsets: int32 [256, 3], P('bond'), may hold values from -4 to 4, as said below
- intact: int32 [256, 64, 64, 256], P('bond', 'pts'), may hold values 0 or 1
Outputs:
- new_displacement: float32 [3, 64, 64, 256], P(None, 'pts', 'bond')
- new_velocity: float32 [3, 64, 64, 256], P(None, 'pts', 'bond')
Inputs may be any that keep to these rules, and one draw needn't show every extreme that they name: `offsets`: every nonzero lattice shift (a, b, c) with a * a + b * b + c * c <= 16, each exactly once, in an order drawn from the seed.
All inputs are finite; a program needn't handle non-finite values. No bound on the sum of `intact` on one device may be relied on, other than what follows from the above.
Results may differ from a plain program's by a relative error of at most 0.0003.
Values sent between devices are 32-bit elements; how exact they have to be, the bound alone decides.
No kernel may reach another device: no remote copies, remote signals or barrier semaphores. Data moves between devices by JAX's collectives and lax.ppermute only.
A program may use at most 128 MiB of HBM per device.

v0:
```python
import math

import jax
import jax.numpy as jnp
from jax import lax
from jax.sharding import PartitionSpec as P

REACH = 4


SPACING = 6.0
FORCE_SCALE = 8.0
TIME_STEP = 0.5
LANE_PAD = 128


def padded_2(block, sides, width):
    for axis, dim in sides:
        count = lax.axis_size(axis)
        forward = [(i, i + 1) for i in range(count - 1)]
        backward = [(target, source) for source, target in forward]
        low = lax.ppermute(
            lax.slice_in_dim(block, block.shape[dim] - width, None, axis=dim), axis, forward
        )
        high = lax.ppermute(lax.slice_in_dim(block, 0, width, axis=dim), axis, backward)
        block = jnp.concatenate([low, block, high], axis=dim)
    return block


def bond_forces(centre, padded, inside, shift, alive):
    shape = centre.shape
    lower = shift + REACH
    anchor = jnp.zeros((), jnp.int32)
    nearby = lax.dynamic_slice(padded, (anchor, lower[0], lower[1], lower[2]), shape)
    present = lax.dynamic_slice(inside, (lower[0], lower[1], lower[2]), shape[1:]) * alive.astype(
        centre.dtype
    )
    bond_vec = shift.astype(centre.dtype) * SPACING
    length = jnp.sqrt(jnp.sum(bond_vec * bond_vec))
    relative = bond_vec[:, None, None, None] + nearby[:3] - centre[:3]
    stretched = jnp.sqrt(jnp.sum(relative * relative, axis=0))
    strain = (stretched - length) / length
    coupling = 0.5 * (centre[3] + nearby[3]) * present / length
    return relative * (coupling * strain / stretched)


def on_device(displacement, velocity, stiffness, offsets, intact):
    slab_rows = displacement.shape[1]
    own_state = jnp.concatenate([displacement, stiffness[None]], axis=0)
    gathered = lax.all_gather(own_state, "bond", axis=2, tiled=True)
    whole = padded_2(gathered, (("pts", 1),), REACH)
    centre = whole[:, REACH : REACH + slab_rows]
    upper_pad = LANE_PAD - REACH
    padded = jnp.pad(whole, ((0, 0), (0, 0), (REACH, REACH), (REACH, upper_pad)))
    first_row = lax.axis_index("pts") * slab_rows - REACH
    global_rows = first_row + jnp.arange(slab_rows + 2 * REACH, dtype=jnp.int32)
    valid_rows = ((global_rows >= 0) & (global_rows < slab_rows * lax.axis_size("pts"))).astype(
        jnp.float32
    )
    plane = jnp.pad(
        jnp.ones((whole.shape[2], whole.shape[3]), jnp.float32),
        ((REACH, REACH), (REACH, upper_pad)),
    )
    inside = valid_rows[:, None, None] * plane[None]
    group = math.gcd(offsets.shape[0], 8)
    turns = offsets.shape[0] // group
    shift_blocks = offsets.reshape((turns, group, 3))
    alive_blocks = intact.reshape((turns, group) + intact.shape[1:])
    batched = jax.vmap(bond_forces, in_axes=(None, None, None, 0, 0))

    def accumulate(total, pieces):
        shift_block, alive_block = pieces
        terms = batched(centre, padded, inside, shift_block, alive_block)
        return (total + jnp.sum(terms, axis=0), None)

    start_total = jnp.zeros((3,) + centre.shape[1:], jnp.float32)
    total = lax.scan(accumulate, start_total, (shift_blocks, alive_blocks))[0]
    force = lax.psum_scatter(total, "bond", scatter_dimension=2, tiled=True)
    density = FORCE_SCALE * force
    new_velocity = velocity + TIME_STEP * density
    new_displacement = displacement + TIME_STEP * new_velocity
    return (new_displacement, new_velocity)


def solution(mesh):
    return jax.shard_map(
        on_device,
        mesh=mesh,
        in_specs=(
            P(None, "pts", "bond", None),
            P(None, "pts", "bond", None),
            P("pts", "bond", None),
            P("bond", None),
            P("bond", "pts", None, None),
        ),
        out_specs=(P(None, "pts", "bond", None), P(None, "pts", "bond", None)),
        check_vma=False,
    )
```

profile of v0, /device:TPU:2, one launch (start us, length us, event | category | flops | bytes accessed | tf_op | source)
XLA Modules:
  0.0 1274.2 jit_solution(2317009471696406641)
XLA Ops:
  9.2 22.9 %all-gather.2.cloned.1.call-done = f32[4,4,64,256]{3,2,1,0:T(8,128)} async-done(((f32[4,4,32,256]{3,2,1,0:T(8,128)}), f32[4,4,64,256]{3,2,1,0:T(8,128)}) %all-gather.2.cloned.1.call-update) | async-done | bytes 1048592 | tf_op jit(solution)/shard_map/all_gather | solution.py:50
  65.4 1182.9 %while.19 = (s32[]{:T(128)}, f32[3,4,64,256]{3,2,1,0:T(8,128)}, s32[16,8,3]{1,0,2:T(8,128)}, f32[4,12,72,384]{3,2,1,0:T(8,128)}, f32[4,4,64,256]{3,2,1,0:T(8,128...) while((s32[]{:T(128)}, f32[3,4,64,256]{3,2,1,0:T(8,128)}, ...), condition=%wide.region_4.5_spmd.clone, body=%wide.region_0.4_spmd.clone.sunk | while | flops 17830268 | bytes 78250400 | solution.py:77
  66.1 41.2 %while.20 = (s32[]{:T(128)}, f32[4,12,72,384]{3,2,1,0:T(8,128)}, s32[8,4]{0,1:T(4,128)S(1)}, f32[8,4,4,64,256]{4,3,2,1,0:T(8,128)}, s32[]{:T(128)}) while((s32[]{:T(128)}, f32[4,12,72,384]{3,2,1,0:T(8,128)}, s32[8,4]{0,1:T(4,128)S(1)}, f32[8,4,4,64,256]{4,3,2,1,0:T(8,128)}, s32[]{:T(128)}) %tuple.72), condition=%wide.while_cond, body=%wide.while_body.sunk | while | flops 2 | bytes 2098821 | solution.py:34
  140.1 41.2 %while.20 = (s32[]{:T(128)}, f32[4,12,72,384]{3,2,1,0:T(8,128)}, s32[8,4]{0,1:T(4,128)S(1)}, f32[8,4,4,64,256]{4,3,2,1,0:T(8,128)}, s32[]{:T(128)}) while((s32[]{:T(128)}, f32[4,12,72,384]{3,2,1,0:T(8,128)}, s32[8,4]{0,1:T(4,128)S(1)}, f32[8,4,4,64,256]{4,3,2,1,0:T(8,128)}, s32[]{:T(128)}) %tuple.72), condition=%wide.while_cond, body=%wide.while_body.sunk | while | flops 2 | bytes 2098821 | solution.py:34
  181.5 19.9 %while.21 = (s32[]{:T(128)}, f32[12,72,384]{2,1,0:T(8,128)S(1)}, s32[8,3]{0,1:T(4,128)S(1)}, f32[8,4,64,256]{3,2,1,0:T(8,128)S(1)}, s32[]{:T(128)}) while((s32[]{:T(128)}, f32[12,72,384]{2,1,0:T(8,128)S(1)}, s32[8,3]{0,1:T(4,128)S(1)}, f32[8,4,64,256]{3,2,1,0:T(8,128)S(1)}, s32[]{:T(128)}) %tuple.75), condition=%wide.while_cond.1, body=%wide.while_body.1.sunk | while | flops 2 | bytes 524425 | solution.py:35
  214.0 41.2 %while.20 = (s32[]{:T(128)}, f32[4,12,72,384]{3,2,1,0:T(8,128)}, s32[8,4]{0,1:T(4,128)S(1)}, f32[8,4,4,64,256]{4,3,2,1,0:T(8,128)}, s32[]{:T(128)}) while((s32[]{:T(128)}, f32[4,12,72,384]{3,2,1,0:T(8,128)}, s32[8,4]{0,1:T(4,128)S(1)}, f32[8,4,4,64,256]{4,3,2,1,0:T(8,128)}, s32[]{:T(128)}) %tuple.72), condition=%wide.while_cond, body=%wide.while_body.sunk | while | flops 2 | bytes 2098821 | solution.py:34
  255.4 19.9 %while.21 = (s32[]{:T(128)}, f32[12,72,384]{2,1,0:T(8,128)S(1)}, s32[8,3]{0,1:T(4,128)S(1)}, f32[8,4,64,256]{3,2,1,0:T(8,128)S(1)}, s32[]{:T(128)}) while((s32[]{:T(128)}, f32[12,72,384]{2,1,0:T(8,128)S(1)}, s32[8,3]{0,1:T(4,128)S(1)}, f32[8,4,64,256]{3,2,1,0:T(8,128)S(1)}, s32[]{:T(128)}) %tuple.75), condition=%wide.while_cond.1, body=%wide.while_body.1.sunk | while | flops 2 | bytes 524425 | solution.py:35
  287.9 41.2 %while.20 = (s32[]{:T(128)}, f32[4,12,72,384]{3,2,1,0:T(8,128)}, s32[8,4]{0,1:T(4,128)S(1)}, f32[8,4,4,64,256]{4,3,2,1,0:T(8,128)}, s32[]{:T(128)}) while((s32[]{:T(128)}, f32[4,12,72,384]{3,2,1,0:T(8,128)}, s32[8,4]{0,1:T(4,128)S(1)}, f32[8,4,4,64,256]{4,3,2,1,0:T(8,128)}, s32[]{:T(128)}) %tuple.72), condition=%wide.while_cond, body=%wide.while_body.sunk | while | flops 2 | bytes 2098821 | solution.py:34
  361.8 41.2 %while.20 = (s32[]{:T(128)}, f32[4,12,72,384]{3,2,1,0:T(8,128)}, s32[8,4]{0,1:T(4,128)S(1)}, f32[8,4,4,64,256]{4,3,2,1,0:T(8,128)}, s32[]{:T(128)}) while((s32[]{:T(128)}, f32[4,12,72,384]{3,2,1,0:T(8,128)}, s32[8,4]{0,1:T(4,128)S(1)}, f32[8,4,4,64,256]{4,3,2,1,0:T(8,128)}, s32[]{:T(128)}) %tuple.72), condition=%wide.while_cond, body=%wide.while_body.sunk | while | flops 2 | bytes 2098821 | solution.py:34
  435.8 41.2 %while.20 = (s32[]{:T(128)}, f32[4,12,72,384]{3,2,1,0:T(8,128)}, s32[8,4]{0,1:T(4,128)S(1)}, f32[8,4,4,64,256]{4,3,2,1,0:T(8,128)}, s32[]{:T(128)}) while((s32[]{:T(128)}, f32[4,12,72,384]{3,2,1,0:T(8,128)}, s32[8,4]{0,1:T(4,128)S(1)}, f32[8,4,4,64,256]{4,3,2,1,0:T(8,128)}, s32[]{:T(128)}) %tuple.72), condition=%wide.while_cond, body=%wide.while_body.sunk | while | flops 2 | bytes 2098821 | solution.py:34
  477.2 19.9 %while.21 = (s32[]{:T(128)}, f32[12,72,384]{2,1,0:T(8,128)S(1)}, s32[8,3]{0,1:T(4,128)S(1)}, f32[8,4,64,256]{3,2,1,0:T(8,128)S(1)}, s32[]{:T(128)}) while((s32[]{:T(128)}, f32[12,72,384]{2,1,0:T(8,128)S(1)}, s32[8,3]{0,1:T(4,128)S(1)}, f32[8,4,64,256]{3,2,1,0:T(8,128)S(1)}, s32[]{:T(128)}) %tuple.75), condition=%wide.while_cond.1, body=%wide.while_body.1.sunk | while | flops 2 | bytes 524425 | solution.py:35
  509.7 41.2 %while.20 = (s32[]{:T(128)}, f32[4,12,72,384]{3,2,1,0:T(8,128)}, s32[8,4]{0,1:T(4,128)S(1)}, f32[8,4,4,64,256]{4,3,2,1,0:T(8,128)}, s32[]{:T(128)}) while((s32[]{:T(128)}, f32[4,12,72,384]{3,2,1,0:T(8,128)}, s32[8,4]{0,1:T(4,128)S(1)}, f32[8,4,4,64,256]{4,3,2,1,0:T(8,128)}, s32[]{:T(128)}) %tuple.72), condition=%wide.while_cond, body=%wide.while_body.sunk | while | flops 2 | bytes 2098821 | solution.py:34
  551.1 19.9 %while.21 = (s32[]{:T(128)}, f32[12,72,384]{2,1,0:T(8,128)S(1)}, s32[8,3]{0,1:T(4,128)S(1)}, f32[8,4,64,256]{3,2,1,0:T(8,128)S(1)}, s32[]{:T(128)}) while((s32[]{:T(128)}, f32[12,72,384]{2,1,0:T(8,128)S(1)}, s32[8,3]{0,1:T(4,128)S(1)}, f32[8,4,64,256]{3,2,1,0:T(8,128)S(1)}, s32[]{:T(128)}) %tuple.75), condition=%wide.while_cond.1, body=%wide.while_body.1.sunk | while | flops 2 | bytes 524425 | solution.py:35
  583.6 41.2 %while.20 = (s32[]{:T(128)}, f32[4,12,72,384]{3,2,1,0:T(8,128)}, s32[8,4]{0,1:T(4,128)S(1)}, f32[8,4,4,64,256]{4,3,2,1,0:T(8,128)}, s32[]{:T(128)}) while((s32[]{:T(128)}, f32[4,12,72,384]{3,2,1,0:T(8,128)}, s32[8,4]{0,1:T(4,128)S(1)}, f32[8,4,4,64,256]{4,3,2,1,0:T(8,128)}, s32[]{:T(128)}) %tuple.72), condition=%wide.while_cond, body=%wide.while_body.sunk | while | flops 2 | bytes 2098821 | solution.py:34
  625.0 19.9 %while.21 = (s32[]{:T(128)}, f32[12,72,384]{2,1,0:T(8,128)S(1)}, s32[8,3]{0,1:T(4,128)S(1)}, f32[8,4,64,256]{3,2,1,0:T(8,128)S(1)}, s32[]{:T(128)}) while((s32[]{:T(128)}, f32[12,72,384]{2,1,0:T(8,128)S(1)}, s32[8,3]{0,1:T(4,128)S(1)}, f32[8,4,64,256]{3,2,1,0:T(8,128)S(1)}, s32[]{:T(128)}) %tuple.75), condition=%wide.while_cond.1, body=%wide.while_body.1.sunk | while | flops 2 | bytes 524425 | solution.py:35
  657.6 41.2 %while.20 = (s32[]{:T(128)}, f32[4,12,72,384]{3,2,1,0:T(8,128)}, s32[8,4]{0,1:T(4,128)S(1)}, f32[8,4,4,64,256]{4,3,2,1,0:T(8,128)}, s32[]{:T(128)}) while((s32[]{:T(128)}, f32[4,12,72,384]{3,2,1,0:T(8,128)}, s32[8,4]{0,1:T(4,128)S(1)}, f32[8,4,4,64,256]{4,3,2,1,0:T(8,128)}, s32[]{:T(128)}) %tuple.72), condition=%wide.while_cond, body=%wide.while_body.sunk | while | flops 2 | bytes 2098821 | solution.py:34
  731.5 41.2 %while.20 = (s32[]{:T(128)}, f32[4,12,72,384]{3,2,1,0:T(8,128)}, s32[8,4]{0,1:T(4,128)S(1)}, f32[8,4,4,64,256]{4,3,2,1,0:T(8,128)}, s32[]{:T(128)}) while((s32[]{:T(128)}, f32[4,12,72,384]{3,2,1,0:T(8,128)}, s32[8,4]{0,1:T(4,128)S(1)}, f32[8,4,4,64,256]{4,3,2,1,0:T(8,128)}, s32[]{:T(128)}) %tuple.72), condition=%wide.while_cond, body=%wide.while_body.sunk | while | flops 2 | bytes 2098821 | solution.py:34
  805.4 41.2 %while.20 = (s32[]{:T(128)}, f32[4,12,72,384]{3,2,1,0:T(8,128)}, s32[8,4]{0,1:T(4,128)S(1)}, f32[8,4,4,64,256]{4,3,2,1,0:T(8,128)}, s32[]{:T(128)}) while((s32[]{:T(128)}, f32[4,12,72,384]{3,2,1,0:T(8,128)}, s32[8,4]{0,1:T(4,128)S(1)}, f32[8,4,4,64,256]{4,3,2,1,0:T(8,128)}, s32[]{:T(128)}) %tuple.72), condition=%wide.while_cond, body=%wide.while_body.sunk | while | flops 2 | bytes 2098821 | solution.py:34
  846.8 19.9 %while.21 = (s32[]{:T(128)}, f32[12,72,384]{2,1,0:T(8,128)S(1)}, s32[8,3]{0,1:T(4,128)S(1)}, f32[8,4,64,256]{3,2,1,0:T(8,128)S(1)}, s32[]{:T(128)}) while((s32[]{:T(128)}, f32[12,72,384]{2,1,0:T(8,128)S(1)}, s32[8,3]{0,1:T(4,128)S(1)}, f32[8,4,64,256]{3,2,1,0:T(8,128)S(1)}, s32[]{:T(128)}) %tuple.75), condition=%wide.while_cond.1, body=%wide.while_body.1.sunk | while | flops 2 | bytes 524425 | solution.py:35
  879.4 41.2 %while.20 = (s32[]{:T(128)}, f32[4,12,72,384]{3,2,1,0:T(8,128)}, s32[8,4]{0,1:T(4,128)S(1)}, f32[8,4,4,64,256]{4,3,2,1,0:T(8,128)}, s32[]{:T(128)}) while((s32[]{:T(128)}, f32[4,12,72,384]{3,2,1,0:T(8,128)}, s32[8,4]{0,1:T(4,128)S(1)}, f32[8,4,4,64,256]{4,3,2,1,0:T(8,128)}, s32[]{:T(128)}) %tuple.72), condition=%wide.while_cond, body=%wide.while_body.sunk | while | flops 2 | bytes 2098821 | solution.py:34
  953.3 41.2 %while.20 = (s32[]{:T(128)}, f32[4,12,72,384]{3,2,1,0:T(8,128)}, s32[8,4]{0,1:T(4,128)S(1)}, f32[8,4,4,64,256]{4,3,2,1,0:T(8,128)}, s32[]{:T(128)}) while((s32[]{:T(128)}, f32[4,12,72,384]{3,2,1,0:T(8,128)}, s32[8,4]{0,1:T(4,128)S(1)}, f32[8,4,4,64,256]{4,3,2,1,0:T(8,128)}, s32[]{:T(128)}) %tuple.72), condition=%wide.while_cond, body=%wide.while_body.sunk | while | flops 2 | bytes 2098821 | solution.py:34
  1027.2 41.2 %while.20 = (s32[]{:T(128)}, f32[4,12,72,384]{3,2,1,0:T(8,128)}, s32[8,4]{0,1:T(4,128)S(1)}, f32[8,4,4,64,256]{4,3,2,1,0:T(8,128)}, s32[]{:T(128)}) while((s32[]{:T(128)}, f32[4,12,72,384]{3,2,1,0:T(8,128)}, s32[8,4]{0,1:T(4,128)S(1)}, f32[8,4,4,64,256]{4,3,2,1,0:T(8,128)}, s32[]{:T(128)}) %tuple.72), condition=%wide.while_cond, body=%wide.while_body.sunk | while | flops 2 | bytes 2098821 | solution.py:34
  1101.2 41.2 %while.20 = (s32[]{:T(128)}, f32[4,12,72,384]{3,2,1,0:T(8,128)}, s32[8,4]{0,1:T(4,128)S(1)}, f32[8,4,4,64,256]{4,3,2,1,0:T(8,128)}, s32[]{:T(128)}) while((s32[]{:T(128)}, f32[4,12,72,384]{3,2,1,0:T(8,128)}, s32[8,4]{0,1:T(4,128)S(1)}, f32[8,4,4,64,256]{4,3,2,1,0:T(8,128)}, s32[]{:T(128)}) %tuple.72), condition=%wide.while_cond, body=%wide.while_body.sunk | while | flops 2 | bytes 2098821 | solution.py:34
  1175.1 41.2 %while.20 = (s32[]{:T(128)}, f32[4,12,72,384]{3,2,1,0:T(8,128)}, s32[8,4]{0,1:T(4,128)S(1)}, f32[8,4,4,64,256]{4,3,2,1,0:T(8,128)}, s32[]{:T(128)}) while((s32[]{:T(128)}, f32[4,12,72,384]{3,2,1,0:T(8,128)}, s32[8,4]{0,1:T(4,128)S(1)}, f32[8,4,4,64,256]{4,3,2,1,0:T(8,128)}, s32[]{:T(128)}) %tuple.72), condition=%wide.while_cond, body=%wide.while_body.sunk | while | flops 2 | bytes 2098821 | solution.py:34
  (1195 shorter events, 1431.2 us)
Async XLA Ops:
  7.2 24.9 %all-gather.2.cloned.1.call-start = ((), (), s32[]{:S(2)}) async-start(), calls=%async_computation.1 | async-start | bytes 1572864 | tf_op jit(solution)/shard_map/all_gather | solution.py:50
  9.1 1256.0 %reduce-scatter.2.cloned.1.call-start = ((), (), s32[]{:S(2)}) async-start(), calls=%async_computation.2 | async-start | bytes 1179648 | tf_op jit(solution)/shard_map/reduce_scatter | solution.py:78
  32.1 14.5 %collective-permute-start.1 = (f32[4,4,64,256]{3,2,1,0:T(8,128)}, f32[4,4,64,256]{3,2,1,0:T(8,128)S(1)}, u32[]{:S(2)}, u32[]{:S(2)}) collective-permute-start(f32[4,4,64,256]{3,2,1,0:T(8,128)} %all-gather.2.cloned.1.call-done), channel_id=1, source_target_pairs={{2,0},{4,2},{6,4},{8,6},{10,8},{12,10},{14,12},{16,14},{18,16},{20... | collective-permute-start | bytes 3145736 | tf_op jit(solution)/shard_map/ppermute | solution.py:25
  34.0 26.4 %collective-permute-start = (f32[4,4,64,256]{3,2,1,0:T(8,128)}, f32[4,4,64,256]{3,2,1,0:T(8,128)S(1)}, u32[]{:S(2)}, u32[]{:S(2)}) collective-permute-start(f32[4,4,64,256]{3,2,1,0:T(8,128)} %all-gather.2.cloned.1.call-done), channel_id=1, source_target_pairs={{0,2},{2,4},{4,6},{6,8},{8,10},{10,12},{12,14},{14,16},{16,18},{18... | collective-permute-start | bytes 3145736 | tf_op jit(solution)/shard_map/ppermute | solution.py:22
  128.8 5.3 copy-start
  136.9 1.3 copy-start.1
  202.7 5.3 copy-start
  276.6 5.3 copy-start
  350.6 5.3 copy-start
  358.6 1.3 copy-start.1
  424.5 5.3 copy-start
  432.6 1.3 copy-start.1
  498.4 5.3 copy-start
  572.4 5.3 copy-start
  646.3 5.3 copy-start
  654.4 1.3 copy-start.1
  720.2 5.3 copy-start
  794.2 5.3 copy-start
  868.1 5.3 copy-start
  942.0 5.3 copy-start
  1016.0 5.3 copy-start
  1089.9 5.3 copy-start
  1163.9 5.3 copy-start
  1237.8 5.3 copy-start
  (28 other events, 29.2 us)
Sparse Core Ops, SparseCore 0:
  9.5 22.4 all-gather.1
  1248.4 16.6 reduce-scatter.1
where the time goes:
time: 1290 us; the launch traced here: 1270 us
  local copies, waits for them, and re-layouts  1040 us (81%)
  other arithmetic  150 us (12%)
  waiting for transfers between devices  62.2 us (5%)
  between operations  14.1 us (1%)
    gather x768, local copies, waits for them, and re-layouts  975 us
    reduce_sum x16, other arithmetic, bond_forces(): stretched = jnp.sqrt(jnp.sum(relative * relative, axis=0))  68.4 us
    mul x16, other arithmetic, bond_forces(): return relative * (coupling * strain / stretched)  44.4 us
  transfers between devices with their start and end apart: 4, of which 4 were waited for; matrix products, arithmetic and copies ran while one was open for 0% of the time, Pallas kernels for 0%

commit v1 on v0

v1 whole, which is shorter than its diff:
```python
import functools
import math

import jax
import jax.numpy as jnp
from jax import lax
from jax.experimental import pallas as pl
from jax.experimental.pallas import tpu as pltpu
from jax.sharding import PartitionSpec as P

REACH = 4
SPACING = 6.0
FORCE_SCALE = 8.0
TIME_STEP = 0.5
LANES = 128
TILE = 8
BLOCK_ROWS = 16
UNROLL = 4


def plane_reach(c):
    return math.isqrt(REACH * REACH - c * c)


def copy_bases(slab):
    bases, total = [], 0
    for c in range(-REACH, REACH + 1):
        bases.append(total + plane_reach(c))
        total += slab + 2 * plane_reach(c)
    return bases, total


def build_tables(state, copies, outside, px, py, slab, rows, halves):
    stride = rows + TILE
    bases, total = copy_bases(slab)
    zero = jnp.zeros((TILE, LANES), jnp.float32)
    lane = lax.broadcasted_iota(jnp.int32, (TILE, LANES), 1)
    row = lax.broadcasted_iota(jnp.int32, (TILE, LANES), 0)

    def clear(n, carry):
        copies[pl.ds(pl.multiple_of(n * stride, TILE), TILE), :] = zero
        return carry

    lax.fori_loop(0, total * 4 * halves + 1, clear, 0, unroll=4)
    for c in range(-REACH, REACH + 1):
        reach = plane_reach(c)

        def one_plane(t, carry, c=c, reach=reach):
            source = t + REACH - reach
            first = (bases[c + REACH] - reach + t) * (4 * halves)
            for field in range(4):
                for tile in range(rows // TILE):
                    parts = [
                        state[field, source, tile * TILE : (tile + 1) * TILE, h * LANES : (h + 1) * LANES]
                        for h in range(halves)
                    ]
                    if field == 2 and c != 0:
                        parts = [part + SPACING * c for part in parts]
                    if c != 0:
                        turned = [pltpu.roll(part, (-c) % LANES, 1) for part in parts]
                        parts = []
                        for h in range(halves):
                            if c > 0:
                                other = turned[h + 1] if h + 1 < halves else None
                                keep = lane < LANES - c
                            else:
                                other = turned[h - 1] if h > 0 else None
                                keep = lane >= -c
                            parts.append(turned[h] if other is None else jnp.where(keep, turned[h], other))
                    for h in range(halves):
                        at = (first + field * halves + h) * stride + TILE + tile * TILE
                        copies[pl.ds(pl.multiple_of(at, TILE), TILE), :] = parts[h]
            return carry

        lax.fori_loop(0, slab + 2 * reach, one_plane, 0)
        for h in range(halves):
            z = lane + (h * LANES + c)
            z_out = (z < 0) | (z >= halves * LANES)
            for tile in range(-1, rows // TILE + 1):
                r = row + tile * TILE
                out = z_out | (r < 0) | (r >= rows)
                at = ((c + REACH) * halves + h) * (rows + 2 * TILE) + (tile + 1) * TILE
                outside[at : at + TILE, :] = out.astype(jnp.int32)

    def one_tile(n, carry):
        tiles = rows // TILE
        plane = n // (halves * tiles)
        tile = n % tiles
        at = pl.multiple_of(tile * TILE, TILE)
        for h in range(halves):
            ux = state[0, REACH + plane, pl.ds(at, TILE), h * LANES : (h + 1) * LANES]
            uy = state[1, REACH + plane, pl.ds(at, TILE), h * LANES : (h + 1) * LANES]
            for s in range(2 * REACH + 1):
                to = ((s * slab + plane) * halves + h) * rows + tile * TILE
                px[pl.ds(pl.multiple_of(to, TILE), TILE), :] = ux - SPACING * (s - REACH)
                py[pl.ds(pl.multiple_of(to, TILE), TILE), :] = uy - SPACING * (s - REACH)
        return carry

    def plane_tiles(n, carry):
        tiles = rows // TILE
        return one_tile((n // tiles) * (halves * tiles) + n % tiles, carry)

    lax.fori_loop(0, slab * (rows // TILE), plane_tiles, 0)


def force_kernel(index, invlen, coef, state, mask, out, copies, outside, px, py, *, slab, rows, halves, count, unroll):
    i = pl.program_id(0)
    block = pl.program_id(1)

    @pl.when((i == 0) & (block == 0))
    def _():
        build_tables(state, copies, outside, px, py, slab, rows, halves)

    stride = rows + TILE
    block_rows = mask.shape[2]
    units = [(tile, h) for tile in range(block_rows // TILE) for h in range(halves)]
    row0 = block * block_rows
    own = {}
    for tile, h in units:
        at = pl.multiple_of(row0 + tile * TILE, TILE)
        own[tile, h] = [
            state[f, REACH + i, pl.ds(at, TILE), h * LANES : (h + 1) * LANES] for f in (2, 3)
        ]
    plane_step = i * (4 * halves * stride) + row0
    own_step = i * (halves * rows) + row0

    def step(g, totals):
        totals = list(totals)
        for u in range(unroll):
            k = g * unroll + u
            q = index[0, k] + plane_step
            o = index[1, k] + row0
            ax = index[2, k] + own_step
            ay = index[3, k] + own_step
            inverse = invlen[k]
            weight = coef[i, k]
            for n, (tile, h) in enumerate(units):
                def near(field):
                    return copies[pl.ds(q + ((field * halves + h) * stride + tile * TILE), TILE), :]

                pz, kp = own[tile, h]
                rx = near(0) - px[pl.ds(pl.multiple_of(ax + (h * rows + tile * TILE), TILE), TILE), :]
                ry = near(1) - py[pl.ds(pl.multiple_of(ay + (h * rows + tile * TILE), TILE), TILE), :]
                rz = near(2) - pz
                inv = lax.rsqrt(rx * rx + ry * ry + rz * rz)
                gone = outside[pl.ds(o + (h * (rows + 2 * TILE) + tile * TILE), TILE), :]
                alive = mask[k, 0, tile * TILE : (tile + 1) * TILE, h * LANES : (h + 1) * LANES]
                factor = jnp.where(alive > gone, weight, 0.0)
                w = (inverse - inv) * (near(3) + kp) * factor
                totals[3 * n] += w * rx
                totals[3 * n + 1] += w * ry
                totals[3 * n + 2] += w * rz
        return tuple(totals)

    zero = jnp.zeros((TILE, LANES), jnp.float32)
    totals = lax.fori_loop(0, count // unroll, step, (zero,) * (3 * len(units)))
    for n, (tile, h) in enumerate(units):
        for f in range(3):
            out[f, 0, tile * TILE : (tile + 1) * TILE, h * LANES : (h + 1) * LANES] = totals[3 * n + f]


def bond_tables(offsets, slab, rows, halves):
    stride = rows + TILE
    bases, _ = copy_bases(slab)
    shift = offsets.astype(jnp.int32)
    a, b, c = shift[:, 0], shift[:, 1], shift[:, 2]
    base = jnp.zeros_like(c)
    for s in range(-REACH, REACH + 1):
        base = jnp.where(c == s, bases[s + REACH], base)
    index = jnp.stack(
        [
            (base + a) * (4 * halves * stride) + TILE + b,
            (c + REACH) * (halves * (rows + 2 * TILE)) + TILE + b,
            (a + REACH) * (slab * halves * rows),
            (b + REACH) * (slab * halves * rows),
        ]
    )
    inverse = 1.0 / (SPACING * jnp.sqrt((a * a + b * b + c * c).astype(jnp.float32)))
    plane = lax.axis_index("pts") * slab + jnp.arange(slab, dtype=jnp.int32)[:, None] + a[None]
    valid = (plane >= 0) & (plane < slab * lax.axis_size("pts"))
    coef = jnp.where(valid, 0.5 * FORCE_SCALE * TIME_STEP * inverse[None], 0.0)
    return index, inverse, coef


def forces(index, inverse, coef, state, intact):
    _, padded, rows, width = state.shape
    slab, count = intact.shape[1], intact.shape[0]
    halves = width // LANES
    _, total = copy_bases(slab)
    block_rows = math.gcd(rows, BLOCK_ROWS)
    unroll = math.gcd(count, UNROLL)
    body = functools.partial(
        force_kernel, slab=slab, rows=rows, halves=halves, count=count, unroll=unroll
    )
    smem = pl.BlockSpec(memory_space=pltpu.SMEM)
    return pl.pallas_call(
        body,
        out_shape=jax.ShapeDtypeStruct((3, slab, rows, width), jnp.float32),
        grid=(slab, rows // block_rows),
        in_specs=[
            smem,
            smem,
            smem,
            pl.BlockSpec(state.shape, lambda i, j: (0, 0, 0, 0), pipeline_mode=pl.Buffered(1)),
            pl.BlockSpec((count, 1, block_rows, width), lambda i, j: (0, i, j, 0)),
        ],
        out_specs=pl.BlockSpec((3, 1, block_rows, width), lambda i, j: (0, i, j, 0)),
        scratch_shapes=[
            pltpu.VMEM((total * 4 * halves * (rows + TILE) + TILE, LANES), jnp.float32),
            pltpu.VMEM(((2 * REACH + 1) * halves * (rows + 2 * TILE), LANES), jnp.int32),
            pltpu.VMEM(((2 * REACH + 1) * slab * halves * rows, LANES), jnp.float32),
            pltpu.VMEM(((2 * REACH + 1) * slab * halves * rows, LANES), jnp.float32),
        ],
        compiler_params=pltpu.CompilerParams(
            dimension_semantics=("arbitrary", "arbitrary"), vmem_limit_bytes=62 * 1024 * 1024
        ),
        name="bonds",
    )(index, inverse, coef, state, intact)


def gather_rows(block, axis, dim):
    count = lax.axis_size(axis)
    me = lax.axis_index(axis)
    width = block.shape[dim]
    shape = list(block.shape)
    shape[dim] = width * count
    whole = lax.dynamic_update_slice_in_dim(jnp.zeros(shape, block.dtype), block, me * width, dim)
    for s in range(1, count):
        other = lax.ppermute(block, axis, [(j, (j + s) % count) for j in range(count)])
        whole = lax.dynamic_update_slice_in_dim(whole, other, (me - s) % count * width, dim)
    return whole


def scatter_rows(block, axis, dim):
    count = lax.axis_size(axis)
    me = lax.axis_index(axis)
    width = block.shape[dim] // count
    total = lax.dynamic_slice_in_dim(block, me * width, width, dim)
    for s in range(1, count):
        part = lax.dynamic_slice_in_dim(block, (me + s) % count * width, width, dim)
        total = total + lax.ppermute(part, axis, [(j, (j + s) % count) for j in range(count)])
    return total


def on_device(displacement, velocity, stiffness, offsets, intact):
    slab = displacement.shape[1]
    own = jnp.concatenate([displacement, stiffness[None]], axis=0)
    whole = gather_rows(own, "bond", 2)
    count = lax.axis_size("pts")
    forward = [(i, i + 1) for i in range(count - 1)]
    low = lax.ppermute(whole[:, slab - REACH :], "pts", forward)
    high = lax.ppermute(whole[:, :REACH], "pts", [(t, s) for s, t in forward])
    state = jnp.concatenate([low, whole, high], axis=1)
    index, inverse, coef = bond_tables(offsets, slab, state.shape[2], state.shape[3] // LANES)
    partial = forces(index, inverse, coef, state, intact)
    new_velocity = velocity + scatter_rows(partial, "bond", 2)
    new_displacement = displacement + TIME_STEP * new_velocity
    return (new_displacement, new_velocity)


def solution(mesh):
    return jax.shard_map(
        on_device,
        mesh=mesh,
        in_specs=(
            P(None, "pts", "bond", None),
            P(None, "pts", "bond", None),
            P("pts", "bond", None),
            P("bond", None),
            P("bond", "pts", None, None),
        ),
        out_specs=(P(None, "pts", "bond", None), P(None, "pts", "bond", None)),
        check_vma=False,
    )
```

time: 1290 us -> 105 us (0.08); the launches traced: 1270 us -> 105 us
  local copies, waits for them, and re-layouts: 1040 us -> 1.18 us
  other arithmetic: 150 us -> 6.89 us
  Pallas kernels: 0 us -> 48.9 us
  waiting for transfers between devices: 62.2 us -> 38.3 us
  between operations: 14.1 us -> 0.73 us
    gather x768 -> x0, local copies, waits for them, and re-layouts: 975 us -> none
    reduce_sum x48 -> x0, other arithmetic: 88.6 us -> none  [the longest x16 68.4 us: bond_forces(): stretched = jnp.sqrt(jnp.sum(relative * relative, axis=0))]
    pallas_call x0 -> x1, Pallas kernels: none -> 48.9 us  [forces(): pl.pallas_call(body, out_shape=jax.ShapeDtypeStruct((3, slab, rows, width...]
    mul x48 -> x1, other arithmetic: 46.9 us -> 0.5 us  [bond_tables(): coef = jnp.where(valid, 0.5 * FORCE_SCALE * TIME_STEP * inverse[None], 0.0)]
    all_gather x1 -> x0, waiting for transfers between devices: 22.9 us -> none  [on_device(): gathered = lax.all_gather(own_state, 'bond', axis=2, tiled=True)]
    slice x16 -> x0, local copies, waits for them, and re-layouts: 19.3 us -> none  [bond_forces(): relative = bond_vec[:, None, None, None] + nearby[:3] - centre[:3]]
    reduce_scatter x1 -> x0, waiting for transfers between devices: 16.8 us -> none  [on_device(): force = lax.psum_scatter(total, 'bond', scatter_dimension=2, tiled=True)]
    ppermute x2 -> x4, waiting for transfers between devices: 22.5 us -> 38.3 us  [the longest x1 20 us: on_device(): low = lax.ppermute(whole[:, slab - REACH:], 'pts', forward)]
  transfers between devices with their start and end apart: 4 -> 4, of which waited for: 4 -> 3; matrix products, arithmetic and copies ran while one was open for 0% -> 2% of each run, Pallas kernels for 0% -> 0%
where the time goes in v1:
time: 105 us
  Pallas kernels  48.9 us (47%)
  waiting for transfers between devices  38.3 us (36%)
  starting transfers between devices  8.76 us (8%)
  other arithmetic  6.89 us (7%)
  local copies, waits for them, and re-layouts  1.18 us (1%)
    pallas_call x1, Pallas kernels, forces(): pl.pallas_call(body, out_shape=jax.ShapeDtypeStruct((3, slab, rows, width...  48.9 us
    ppermute x1, waiting for transfers between devices, on_device(): low = lax.ppermute(whole[:, slab - REACH:], 'pts', forward)  20 us
    ppermute x1, waiting for transfers between devices, gather_rows(): lax.ppermute(block, axis, [(j, (j + s) % count) for j in range(count)])  12.1 us
    ppermute x1, waiting for transfers between devices, scatter_rows(): lax.ppermute(part, axis, [(j, (j + s) % count) for j in range(count)])  6.23 us
    ppermute x1, starting transfers between devices, on_device(): high = lax.ppermute(whole[:, :REACH], 'pts', [(t, s) for s, t in forward])  3.64 us
  transfers between devices with their start and end apart: 4, of which 3 were waited for; matrix products, arithmetic and copies ran while one was open for 2% of the time, Pallas kernels for 0%

profile of v1, /device:TPU:2, one launch (start us, length us, event | category | flops | bytes accessed | tf_op | source)
XLA Modules:
  0.0 104.8 jit_solution(16639253079011692287)
XLA Ops:
  0.6 0.0 copy-start.2
  0.6 0.1 broadcast_in_dim.56
  0.7 1.2 %pad_maximum_fusion.1 = (f32[4,4,32,256]{3,2,1,0:T(8,128)S(1)}, f32[4,4,64,256]{3,2,1,0:T(8,128)S(1)}) fusion(f32[1,4,32,256]{3,2,1,0:T(8,128)} %bitcast.32, f32[3,4,32,256]{3,2,1,0:T(8,128)} %param.5, f32[4,4,64,256]{3,2,1,0:T(8,128)S(1)} %broadcast_in_dim.56, s32[]{:T(128)S(6)} %select_n.125), kind=kLoop, calls=%fused_computation.1 | loop fusion | flops 131072 | bytes 1572868 | tf_op jit(solution)/shard_map/concatenate | solution.py:247
  1.9 1.6 %collective-permute-start = (f32[4,4,32,256]{3,2,1,0:T(8,128)S(1)}, f32[4,4,32,256]{3,2,1,0:T(8,128)S(1)}, u32[]{:S(2)}, u32[]{:S(2)}) collective-permute-start(f32[4,4,32,256]{3,2,1,0:T(8,128)S(1)} %get-tuple-element.6), channel_id=1, source_target_pairs={{0,1},{1,0},{2,3},{3,2},{4,5},{5,4},{6,7},{7,6},{8,9},{9,8},{10,11... | collective-permute-start | bytes 1572872 | tf_op jit(solution)/shard_map/ppermute | solution.py:229
  3.5 12.1 %collective-permute-done = f32[4,4,32,256]{3,2,1,0:T(8,128)S(1)} collective-permute-done((f32[4,4,32,256]{3,2,1,0:T(8,128)S(1)}, f32[4,4,32,256]{3,2,1,0:T(8,128)S(1)}, u32[]{:S(2)}, u32[]{:S(2)}) %collective-permute-start) | collective-permute-done | bytes 524320 | tf_op jit(solution)/shard_map/ppermute | solution.py:229
  15.7 1.9 %collective-permute-start.1 = (f32[4,4,64,256]{3,2,1,0:T(8,128)S(1)}, f32[4,4,64,256]{3,2,1,0:T(8,128)S(1)}, u32[]{:S(2)}, u32[]{:S(2)}) collective-permute-start(f32[4,4,64,256]{3,2,1,0:T(8,128)S(1)} %constant_dynamic-update-slice_fusion), channel_id=1, source_target_pairs={{0,2},{2,4},{4,6},{6,8},{8,10},{10,12},{12,14},{14,16},{16,18},{18... | collective-permute-start | bytes 3145736 | tf_op jit(solution)/shard_map/ppermute | solution.py:251
  17.7 3.6 %collective-permute-start.2 = (f32[4,4,64,256]{3,2,1,0:T(8,128)S(1)}, f32[4,4,64,256]{3,2,1,0:T(8,128)S(1)}, u32[]{:S(2)}, u32[]{:S(2)}) collective-permute-start(f32[4,4,64,256]{3,2,1,0:T(8,128)S(1)} %constant_dynamic-update-slice_fusion), channel_id=1, source_target_pairs={{2,0},{4,2},{6,4},{8,6},{10,8},{12,10},{14,12},{16,14},{18,16},{20... | collective-permute-start | bytes 3145736 | tf_op jit(solution)/shard_map/ppermute | solution.py:252
  21.3 0.0 copy-done.2
  21.4 0.6 pad_add_fusion.index
  22.0 0.5 broadcast_multiply_fusion
  22.5 0.6 fusion.1.coef
  23.1 20.0 %collective-permute-done.1 = f32[4,4,64,256]{3,2,1,0:T(8,128)S(1)} collective-permute-done((f32[4,4,64,256]{3,2,1,0:T(8,128)S(1)}, f32[4,4,64,256]{3,2,1,0:T(8,128)S(1)}, u32[]{:S(2)}, u32[]{:S(2)}) %collective-permute-start.1) | collective-permute-done | bytes 1048608 | tf_op jit(solution)/shard_map/ppermute | solution.py:251
  43.1 0.0 collective-permute-done.2
  43.1 1.9 %pad_maximum_fusion.state = f32[4,12,64,256]{3,2,1,0:T(8,128)} fusion(f32[4,4,64,256]{3,2,1,0:T(8,128)S(1)} %collective-permute-done.2, f32[4,4,64,256]{3,2,1,0:T(8,128)S(1)} %constant_dynamic-update-slice_fusion, f32[4,4,64,256]{3,2,1,0:T(8,128)S(1)} %collective-permute-done.1), kind=kLoop, calls=%fused_computation | loop fusion | flops 1572864 | bytes 6291456 | tf_op jit(solution)/shard_map/concatenate | solution.py:253
  45.0 0.0 copy-start
  45.0 0.0 copy-start.1
  45.0 48.9 %bonds.1 = f32[3,4,64,256]{3,2,1,0:T(8,128)} custom-call(s32[4,128]{1,0:T(4,128)} %pad_add_fusion.index, f32[128]{0:T(128)} %get-tuple-element.5.invlen, f32[4,128]{1,0:T(4,128)} %fusion.1.coef, f32[4,12,64,256]{3,2,1,0:T(8,128)} %pad_maximum_fusion.state, s32[128,4,64,256]{3,2,1,0:T(8,128)} %mask.1), custom_call_target="tpu_custom_call" | custom-call | tf_op jit(solution)/shard_map/bonds/pallas_call | solution.py:196
  93.9 1.0 constant_dynamic-slice_fusion
  94.9 1.6 %collective-permute-start.3 = (f32[3,4,32,256]{3,2,1,0:T(8,128)S(1)}, f32[3,4,32,256]{3,2,1,0:T(8,128)S(1)}, u32[]{:S(2)}, u32[]{:S(2)}) collective-permute-start(f32[3,4,32,256]{3,2,1,0:T(8,128)S(1)} %constant_dynamic-slice_fusion), channel_id=1, source_target_pairs={{0,1},{1,0},{2,3},{3,2},{4,5},{5,4},{6,7},{7,6},{8,9},{9,8},{10,11... | collective-permute-start | bytes 1179656 | tf_op jit(solution)/shard_map/ppermute | solution.py:241
  96.5 6.2 %collective-permute-done.3 = f32[3,4,32,256]{3,2,1,0:T(8,128)S(1)} collective-permute-done((f32[3,4,32,256]{3,2,1,0:T(8,128)S(1)}, f32[3,4,32,256]{3,2,1,0:T(8,128)S(1)}, u32[]{:S(2)}, u32[]{:S(2)}) %collective-permute-start.3) | collective-permute-done | bytes 393248 | tf_op jit(solution)/shard_map/ppermute | solution.py:241
  102.8 0.0 copy-done
  102.8 0.0 copy-done.1
  102.8 2.0 %multiply_add_fusion = (f32[3,4,32,256]{3,2,1,0:T(8,128)}, f32[3,4,32,256]{3,2,1,0:T(8,128)}) fusion(f32[3,4,32,256]{3,2,1,0:T(8,128)S(1)} %copy-done, f32[3,4,32,256]{3,2,1,0:T(8,128)S(1)} %copy-done.1, f32[3,4,32,256]{3,2,1,0:T(8,128)S(1)} %collective-permute-done.3, f32[3,4,64,256]{3,2,1,0:T(8,128)} %bonds.1, s32[]{:T(128)S(6)} %select_n.125), kind=kLoop, calls=%fused_computation.2 | loop fusion | flops 393216 | bytes 2359300 | tf_op jit(solution)/shard_map/add | solution.py:257
  (3 shorter events, 0.1 us)
Async XLA Ops:
  0.6 20.7 %copy-start.2 = (s32[128,3]{0,1:T(4,128)S(1)}, s32[128,3]{0,1:T(4,128)}, u32[]{:S(2)}) copy-start(s32[128,3]{0,1:T(4,128)} %param.8) | copy-start | bytes 4612
  1.9 13.7 %collective-permute-start = (f32[4,4,32,256]{3,2,1,0:T(8,128)S(1)}, f32[4,4,32,256]{3,2,1,0:T(8,128)S(1)}, u32[]{:S(2)}, u32[]{:S(2)}) collective-permute-start(f32[4,4,32,256]{3,2,1,0:T(8,128)S(1)} %get-tuple-element.6), channel_id=1, source_target_pairs={{0,1},{1,0},{2,3},{3,2},{4,5},{5,4},{6,7},{7,6},{8,9},{9,8},{10,11... | collective-permute-start | bytes 1572872 | tf_op jit(solution)/shard_map/ppermute | solution.py:229
  15.7 27.4 %collective-permute-start.1 = (f32[4,4,64,256]{3,2,1,0:T(8,128)S(1)}, f32[4,4,64,256]{3,2,1,0:T(8,128)S(1)}, u32[]{:S(2)}, u32[]{:S(2)}) collective-permute-start(f32[4,4,64,256]{3,2,1,0:T(8,128)S(1)} %constant_dynamic-update-slice_fusion), channel_id=1, source_target_pairs={{0,2},{2,4},{4,6},{6,8},{8,10},{10,12},{12,14},{14,16},{16,18},{18... | collective-permute-start | bytes 3145736 | tf_op jit(solution)/shard_map/ppermute | solution.py:251
  17.7 25.4 %collective-permute-start.2 = (f32[4,4,64,256]{3,2,1,0:T(8,128)S(1)}, f32[4,4,64,256]{3,2,1,0:T(8,128)S(1)}, u32[]{:S(2)}, u32[]{:S(2)}) collective-permute-start(f32[4,4,64,256]{3,2,1,0:T(8,128)S(1)} %constant_dynamic-update-slice_fusion), channel_id=1, source_target_pairs={{2,0},{4,2},{6,4},{8,6},{10,8},{12,10},{14,12},{16,14},{18,16},{20... | collective-permute-start | bytes 3145736 | tf_op jit(solution)/shard_map/ppermute | solution.py:252
  45.0 57.8 %copy-start = (f32[3,4,32,256]{3,2,1,0:T(8,128)S(1)}, f32[3,4,32,256]{3,2,1,0:T(8,128)}, u32[]{:S(2)}) copy-start(f32[3,4,32,256]{3,2,1,0:T(8,128)} %param.5) | copy-start | bytes 1179652
  45.0 57.8 %copy-start.1 = (f32[3,4,32,256]{3,2,1,0:T(8,128)S(1)}, f32[3,4,32,256]{3,2,1,0:T(8,128)}, u32[]{:S(2)}) copy-start(f32[3,4,32,256]{3,2,1,0:T(8,128)} %param.6) | copy-start | bytes 1179652
  94.9 7.8 %collective-permute-start.3 = (f32[3,4,32,256]{3,2,1,0:T(8,128)S(1)}, f32[3,4,32,256]{3,2,1,0:T(8,128)S(1)}, u32[]{:S(2)}, u32[]{:S(2)}) collective-permute-start(f32[3,4,32,256]{3,2,1,0:T(8,128)S(1)} %constant_dynamic-slice_fusion), channel_id=1, source_target_pairs={{0,1},{1,0},{2,3},{3,2},{4,5},{5,4},{6,7},{7,6},{8,9},{9,8},{10,11... | collective-permute-start | bytes 1179656 | tf_op jit(solution)/shard_map/ppermute | solution.py:241
